TPU v7x, 32 devices: a whole 2x2x4 slice. The times are simulated.
32 devices in a mesh: grp: 4 (over y, x), bal: 8 (over z, core).
Axes of the slice: x: 2, y: 2, z: 4, core: 2. Of those that a mesh axis runs over, the one named last changes fastest.
Arguments:
- tracers: float32 [2, 64, 16, 2048], P(None, None, 'grp', 'bal'), may hold values from -6 to 6
- winds: bfloat16 [2, 64, 16, 2048], P(None, None, 'grp', 'bal'), may hold values from -16 to 16
- node_mass: float32 [16, 2048], P('grp', 'bal'), may hold values from 0.07 to 5.6
- column_cost: int32 [8, 1024], P('grp', 'bal'), may hold values from 1 to 3, as said below
- weight_in: bfloat16 [256, 1024], replicated, may hold values from -0.375 to 0.375
- weight_out: bfloat16 [1024, 256], replicated, may hold values from -0.1875 to 0.1875
Outputs:
- tracers_next: float32 [2, 64, 16, 2048], P(None, None, 'grp', 'bal')
- columns_out: bfloat16 [4, 64, 8, 1024], P(None, None, 'grp', 'bal')
Inputs may be any that keep to these rules, and one draw needn't show every extreme that they name: `column_cost`: among the columns of one index of grp (rows 2 * g to 2 * g + 1 of all columns), exactly a quarter have cost 3 and exactly a quarter cost 2.
All inputs are finite; a program needn't handle non-finite values.
Results may differ from a plain program's by a relative error of at most 0.008.
Values may be sent and summed in bfloat16 or wider, within the bound.
A program may use at most 64 MiB of HBM per device.

v0:
```python
import jax
import jax.numpy as jnp
from jax import lax
from jax.sharding import PartitionSpec as P

time_step = 0.02
remap_table = ((0.45, 0.4, 0.15, 0.0), (0.0, 0.15, 0.4, 0.45))
gll_points = (-1.0, -0.4472135954999579, 0.4472135954999579, 1.0)


def extended(array, sides, width):
    for axis, dim in sides:
        count, length = (lax.axis_size(axis), array.shape[dim])
        up = [(i, (i + 1) % count) for i in range(count)]
        down = [(j, i) for i, j in up]
        last = lax.slice_in_dim(array, length - width, length, axis=dim)
        leading = lax.slice_in_dim(array, 0, width, axis=dim)
        before = lax.ppermute(last, axis, up)
        after = lax.ppermute(leading, axis, down)
        array = jnp.concatenate([before, array, after], axis=dim)
    return array


def gll_matrix():
    matrix = []
    for row_idx in range(4):
        entries = []
        for col_idx in range(4):
            if row_idx == col_idx:
                running = 0.0
                for third_idx in range(4):
                    if third_idx != row_idx:
                        running += 1.0 / (gll_points[row_idx] - gll_points[third_idx])
                entries.append(2.0 * running)
            else:
                numerator = 1.0
                denominator = 1.0
                for third_idx in range(4):
                    if third_idx != row_idx:
                        numerator *= gll_points[row_idx] - gll_points[third_idx]
                    if third_idx != col_idx:
                        denominator *= gll_points[col_idx] - gll_points[third_idx]
                entries.append(
                    2.0 * numerator / (denominator * (gll_points[row_idx] - gll_points[col_idx]))
                )
        matrix.append(entries)
    return matrix


def derivatives(values):
    derivative = jnp.array(gll_matrix(), jnp.float32)
    layout = values.shape
    blocks_x = values.reshape(layout[:-2] + (layout[-2] // 4, 4, layout[-1]))
    along_x = jnp.einsum(
        "ij,...ejy->...eiy", derivative, blocks_x, precision=lax.Precision.HIGHEST
    ).reshape(layout)
    blocks_y = values.reshape(layout[:-1] + (layout[-1] // 4, 4))
    along_y = jnp.einsum(
        "ij,...ej->...ei", derivative, blocks_y, precision=lax.Precision.HIGHEST
    ).reshape(layout)
    return (along_x, along_y)


def tendency(tracer_vals, wind_vals):
    along_x, along_y = derivatives(tracer_vals)
    speeds = wind_vals.astype(jnp.float32)
    return -(speeds[0] * along_x + speeds[1] * along_y)


def remap_columns(stacked):
    weights_table = jnp.array(remap_table, jnp.float32)
    layout = stacked.shape
    blocks = stacked.reshape(layout[:-2] + (layout[-2] // 4, 4, layout[-1] // 4, 4))
    cell_values = jnp.einsum(
        "pa,qb,...xayb->...xpyq",
        weights_table,
        weights_table,
        blocks,
        precision=lax.Precision.HIGHEST,
    )
    return cell_values.reshape(layout[:-2] + (layout[-2] // 2, layout[-1] // 2))


def network_step(column_state, weight_in, weight_out):
    hidden = jax.nn.gelu(
        jnp.dot(column_state.astype(jnp.bfloat16), weight_in, preferred_element_type=jnp.float32)
    ).astype(jnp.bfloat16)
    return column_state + jnp.dot(hidden, weight_out, preferred_element_type=jnp.float32)


def pass_first(values):
    channels, extent, across = values.shape
    elements = extent // 4
    blocks = values.reshape(channels, elements, 4, across)
    edge_rows = jnp.stack([blocks[:, :, 0], blocks[:, :, 3]], axis=2).reshape(
        channels, 2 * elements, across
    )
    padded = extended(edge_rows.astype(jnp.bfloat16), (("grp", 1),), 1).astype(edge_rows.dtype)
    paired = padded.reshape(channels, elements + 1, 2, across).sum(axis=2)
    rebuilt = jnp.concatenate(
        [paired[:, :-1, None], blocks[:, :, 1:3], paired[:, 1:, None]], axis=2
    )
    return rebuilt.reshape(channels, extent, across)


def pass_second(values):
    channels, extent, across = values.shape
    elements = across // 4
    blocks = values.reshape(channels, extent, elements, 4)
    edge_rows = jnp.stack([blocks[..., 0], blocks[..., 3]], axis=3).reshape(
        channels, extent, 2 * elements
    )
    padded = extended(edge_rows.astype(jnp.bfloat16), (("bal", 2),), 1).astype(edge_rows.dtype)
    paired = padded.reshape(channels, extent, elements + 1, 2).sum(axis=3)
    rebuilt = jnp.concatenate(
        [paired[..., :-1, None], blocks[..., 1:3], paired[..., 1:, None]], axis=3
    )
    return rebuilt.reshape(channels, extent, across)


def home_columns(columns, cost_flat, weight_in, weight_out):
    column_state = columns.astype(jnp.float32)
    for substep in range(3):
        stepped = network_step(column_state, weight_in, weight_out)
        column_state = jnp.where((cost_flat > substep)[:, None], stepped, column_state)
    return column_state.astype(jnp.bfloat16)


def shards(tracers, winds, node_mass, column_cost, weight_in, weight_out):
    levels = tracers.shape[1]
    extent, across = node_mass.shape
    weighted = tendency(tracers, winds) * node_mass
    channels = jnp.concatenate(
        [weighted.reshape(2 * levels, extent, across), node_mass[None]], axis=0
    )
    summed = pass_second(pass_first(channels))
    averaged = summed[:-1] / summed[-1:]
    tracers_next = tracers + time_step * averaged.reshape(tracers.shape)
    stacked = jnp.concatenate([tracers_next, winds.astype(jnp.float32)], axis=0)
    cell_values = remap_columns(stacked).astype(jnp.bfloat16)
    columns = cell_values.reshape(4 * levels, -1).T
    cost_flat = column_cost.reshape(-1)
    result = home_columns(columns, cost_flat, weight_in, weight_out)
    columns_out = result.T.reshape(cell_values.shape)
    return (tracers_next, columns_out)


def solution(mesh):
    placed = (
        P(None, None, "grp", "bal"),
        P(None, None, "grp", "bal"),
        P("grp", "bal"),
        P("grp", "bal"),
        P(),
        P(),
    )
    return jax.shard_map(
        shards,
        mesh=mesh,
        in_specs=placed,
        out_specs=(P(None, None, "grp", "bal"), P(None, None, "grp", "bal")),
        check_vma=False,
    )
```

profile of v0, /device:TPU:0, one launch (start us, length us, event | category | flops | bytes accessed | tf_op | source)
XLA Modules:
  0.0 54.9 jit_solution(13400459457872977134)
XLA Ops:
  1.4 1.4 %copy.53 = f32[2,64,4,256]{1,3,2,0:T(8,128)S(1)} copy(f32[2,64,4,256]{3,2,1,0:T(4,128)} %param.8) | data formatting | bytes 1048576 | tf_op args[0]
  2.8 0.8 %copy.54 = f32[2,64,4,64,4]{3,4,2,1,0:T(4,128)S(1)} copy(f32[2,64,4,64,4]{1,4,3,2,0:T(4,128)S(1)} %bitcast.120) | data formatting | bytes 1048576 | tf_op jit(solution)/shard_map/reshape | solution.py:57
  3.6 1.8 %convolution_bitcast_fusion = f32[2,64,4,64,4]{3,4,2,1,0:T(4,128)S(1)} fusion(f32[4,4,1,1,1]{1,0,4,3,2:T(4,128)S(1)} %copy-done.8, f32[2,64,4,64,4]{3,4,2,1,0:T(4,128)S(1)} %copy.54), kind=kOutput, calls=%fused_computation.4 | convolution fusion | flops 6291456 | bytes 1048640 | tf_op jit(solution)/shard_map/ij,...ej->...ei/dot_general | solution.py:58
  5.5 1.3 %copy.55 = f32[2,64,4,64,4]{1,0,4,3,2:T(2,128)} copy(f32[2,64,4,64,4]{3,4,2,1,0:T(4,128)S(1)} %convolution_bitcast_fusion) | data formatting | bytes 1048576 | tf_op jit(solution)/shard_map/ij,...ej->...ei/dot_general | solution.py:58
  6.8 1.9 %reshape.90 = f32[128,4,256]{0,2,1:T(8,128)S(1)} reshape(f32[2,64,4,64,4]{1,0,4,3,2:T(2,128)} %copy.55) | data formatting | bytes 1048576 | tf_op jit(solution)/shard_map/reshape | solution.py:60
  8.9 1.0 %fusion.83 = f32[4,2,64,256]{3,0,2,1:T(4,128)S(1)} fusion(f32[4,4,1,1]{1,0,3,2:T(4,128)S(1)} %copy-done.7, f32[2,64,4,256]{3,2,1,0:T(4,128)S(1)} %copy-done.1), kind=kOutput, calls=%fused_computation.96 | convolution fusion | flops 6291456 | bytes 1048640 | tf_op jit(solution)/shard_map/ij,...ejy->...eiy/dot_general | solution.py:54
  10.4 1.5 %fusion.76 = (f32[1,64,4,256]{1,0,3,2:T(1,128)S(1)}, f32[1,64,4,256]{1,0,3,2:T(1,128)}) fusion(bf16[2,64,4,256]{1,0,3,2:T(2,128)(2,1)S(1)} %copy.49), kind=kLoop, calls=%fused_computation.90 | loop fusion | bytes 1048576 | tf_op jit(solution)/shard_map/slice | solution.py:67
  11.9 1.2 %copy.52 = f32[64,4,256]{2,0,1:T(8,128)S(1)} copy(f32[64,4,256]{0,2,1:T(8,128)} %bitcast.127) | data formatting | bytes 524288 | tf_op jit(solution)/shard_map/mul | solution.py:67
  13.2 0.9 %copy.50 = f32[64,4,256]{2,0,1:T(8,128)} copy(f32[64,4,256]{0,2,1:T(8,128)S(1)} %bitcast.126) | data formatting | bytes 524288 | tf_op jit(solution)/shard_map/mul | solution.py:67
  14.0 1.1 %fusion.32 = f32[128,4,256]{2,0,1:T(8,128)S(1)} fusion(f32[128,4,256]{2,0,1:T(8,128)S(1)} %copy.56, f32[128,4,256]{2,1,0:T(4,128)S(1)} %bitcast.125, f32[4,256]{1,0:T(4,128)S(1)} %copy-done.5, f32[64,4,256]{2,0,1:T(8,128)S(1)} %copy.52, f32[64,4,256]{2,0,1:T(8,128)} %copy.50), kind=kLoop, calls=%fused_computation.46 | loop fusion | flops 655360 | bytes 2101248 | tf_op jit(solution)/shard_map/mul | solution.py:132
  15.9 3.9 %collective-permute-start.1 = (bf16[129,1,256]{2,0,1:T(8,128)(2,1)}, bf16[129,1,256]{2,0,1:T(8,128)(2,1)S(1)}, u32[]{:S(2)}, u32[]{:S(2)}) collective-permute-start(bf16[129,1,256]{2,0,1:T(8,128)(2,1)} %get-tuple-element.23), channel_id=1, source_target_pairs={{8,0},{16,8},{24,16},{0,24},{9,1},{17,9},{25,17},{1,25},{10,2},{18... | collective-permute-start | bytes 198152 | tf_op jit(solution)/shard_map/ppermute | solution.py:19
  20.5 1.3 %convert_element_type.68 = f32[2,64,4,256]{1,0,3,2:T(2,128)} convert(bf16[2,64,4,256]{1,0,3,2:T(2,128)(2,1)S(1)} %copy.49) | non-fusion elementwise | flops 131072 | bytes 786432 | tf_op jit(solution)/shard_map/convert_element_type | solution.py:66
  22.3 2.7 %collective-permute-done = bf16[129,1,256]{2,0,1:T(8,128)(2,1)S(1)} collective-permute-done((bf16[129,1,256]{2,0,1:T(8,128)(2,1)S(1)}, bf16[129,1,256]{2,0,1:T(8,128)(2,1)S(1)}, u32[]{:S(2)}, u32[]{:S(2)}) %collective-permute-start) | collective-permute-done | bytes 66080 | tf_op jit(solution)/shard_map/ppermute | solution.py:18
  25.5 0.8 %fusion.74 = bf16[129,4,64,4]{0,1,3,2:T(4,128)(2,1)S(1)} fusion(f32[129,1,64,4]{0,1,3,2:T(1,128)S(1)} %bitcast.121, f32[129,2,64,4]{0,1,3,2:T(2,128)S(1)} %bitcast.118, f32[129,1,64,4]{0,1,3,2:T(1,128)S(1)} %bitcast.123), kind=kLoop, calls=%fused_computation.88 | loop fusion | flops 792576 | bytes 792576 | tf_op jit(solution)/shard_map/convert.6
  26.6 1.7 %collective-permute-start.3 = (bf16[129,4,1]{0,1,2:T(4,128)(2,1)S(1)}, bf16[129,4,1]{0,1,2:T(4,128)(2,1)S(1)}, u32[]{:S(2)}, u32[]{:S(2)}) collective-permute-start(bf16[129,4,1]{0,1,2:T(4,128)(2,1)S(1)} %get-tuple-element.21), channel_id=1, source_target_pairs={{1,0},{2,1},{3,2},{4,3},{5,4},{6,5},{7,6},{0,7},{9,8},{10,9},{11,1... | collective-permute-start | bytes 3104 | tf_op jit(solution)/shard_map/ppermute | solution.py:19
  28.3 1.7 %pad_maximum_fusion.1 = f32[129,4,64,4]{0,1,3,2:T(4,128)S(1)} fusion(f32[129,1,64,4]{0,1,3,2:T(1,128)S(1)} %bitcast.122, f32[129,2,64,4]{0,1,3,2:T(2,128)S(1)} %bitcast.119, f32[129,1,64,4]{0,1,3,2:T(1,128)} %bitcast.124), kind=kLoop, calls=%fused_computation.35 | loop fusion | flops 264192 | bytes 1056768 | tf_op jit(solution)/shard_map/concatenate | solution.py:100
  30.1 3.0 %collective-permute-done.2 = bf16[129,4,1]{0,1,2:T(4,128)(2,1)S(1)} collective-permute-done((bf16[129,4,1]{0,1,2:T(4,128)(2,1)S(1)}, bf16[129,4,1]{0,1,2:T(4,128)(2,1)S(1)}, u32[]{:S(2)}, u32[]{:S(2)}) %collective-permute-start.2) | collective-permute-done | bytes 1064 | tf_op jit(solution)/shard_map/ppermute | solution.py:18
  34.5 1.7 %slice.79 = f32[2,64,4,256]{1,0,3,2:T(2,128)} reshape(f32[128,4,64,4]{0,3,2,1:T(4,128)S(1)} %copy.63) | data formatting | bytes 1048576 | tf_op jit(solution)/shard_map/slice | solution.py:137
  36.3 2.9 %multiply_add_fusion = f32[2,64,4,256]{1,0,3,2:T(2,128)S(1)} fusion(f32[2,64,4,256]{1,0,3,2:T(2,128)S(1)} %copy.65, f32[2,64,4,256]{1,0,3,2:T(2,128)} %slice.79, f32[4,256]{1,0:T(4,128)S(1)} %copy.77), kind=kLoop, calls=%fused_computation.38 | loop fusion | flops 393216 | bytes 1576960 | tf_op jit(solution)/shard_map/add | solution.py:138
  39.2 1.2 %copy.71 = f32[2,64,4,256]{3,2,1,0:T(4,128)} copy(f32[2,64,4,256]{1,0,3,2:T(2,128)S(1)} %multiply_add_fusion) | data formatting | bytes 1048576
  40.4 2.5 %pad_maximum_fusion = f32[4,64,4,256]{1,0,3,2:T(4,128)} fusion(f32[2,64,4,256]{1,0,3,2:T(2,128)S(1)} %copy-done.2, f32[2,64,4,256]{1,0,3,2:T(2,128)S(1)} %multiply_add_fusion), kind=kLoop, calls=%fused_computation | loop fusion | flops 262144 | bytes 2097152 | tf_op jit(solution)/shard_map/concatenate | solution.py:139
  42.9 2.9 %copy.67 = f32[4,64,4,64,4]{3,2,4,1,0:T(4,128)S(1)} copy(f32[4,64,4,64,4]{1,0,4,3,2:T(4,128)} %bitcast.117) | data formatting | bytes 2097152 | tf_op jit(solution)/shard_map/reshape.4
  45.9 3.8 %fusion.84 = f32[4,64,64,4,2]{2,4,3,1,0:T(2,128)S(1)} fusion(f32[4,64,4,64,4]{3,2,4,1,0:T(4,128)S(1)} %copy.67, f32[2,4,1,1,1]{1,0,4,3,2:T(2,128)S(1)} %copy-done.6), kind=kOutput, calls=%fused_computation.97 | convolution fusion | flops 6291456 | bytes 1572896 | tf_op jit(solution)/shard_map/pa,qb,...xayb->...xpyq/dot_general | solution.py:74
  49.7 1.9 %fusion = bf16[4,64,1,2,64,2]{4,5,3,1,0,2:T(2,128)(2,1)S(1)} fusion(f32[2,4,1,1,1]{1,0,4,3,2:T(2,128)S(1)} %copy-done.6, f32[4,64,64,4,2]{2,4,3,1,0:T(2,128)S(1)} %fusion.84), kind=kOutput, calls=%fused_computation.6 | convolution fusion | flops 3211264 | bytes 655392 | tf_op jit(solution)/shard_map/pa,qb,...xayb->...xpyq/dot_general | solution.py:74
  (61 shorter events, 8.8 us)
Async XLA Ops:
  0.6 51.5 %copy-start = (bf16[1024,256]{1,0:T(8,128)(2,1)S(1)}, bf16[1024,256]{1,0:T(8,128)(2,1)}, u32[]{:S(2)}) copy-start(bf16[1024,256]{1,0:T(8,128)(2,1)} %param.13) | copy-start | bytes 1572868
  0.6 3.0 %copy-start.8 = (f32[4,4,1,1,1]{1,0,4,3,2:T(4,128)S(1)}, f32[4,4,1,1,1]{1,0,4,3,2:T(4,128)}, u32[]{:S(2)}) copy-start(f32[4,4,1,1,1]{1,0,4,3,2:T(4,128)} %constant.26) | copy-start | bytes 196
  5.4 3.4 %copy-start.1 = (f32[2,64,4,256]{3,2,1,0:T(4,128)S(1)}, f32[2,64,4,256]{3,2,1,0:T(4,128)}, u32[]{:S(2)}) copy-start(f32[2,64,4,256]{3,2,1,0:T(4,128)} %param.8) | copy-start | bytes 1572868
  5.4 3.4 %copy-start.7 = (f32[4,4,1,1]{1,0,3,2:T(4,128)S(1)}, f32[4,4,1,1]{1,0,3,2:T(4,128)}, u32[]{:S(2)}) copy-start(f32[4,4,1,1]{1,0,3,2:T(4,128)} %constant.25) | copy-start | bytes 196
  6.8 3.1 %copy-start.4 = (bf16[2,64,4,256]{3,2,1,0:T(4,128)(2,1)S(1)}, bf16[2,64,4,256]{3,2,1,0:T(4,128)(2,1)}, u32[]{:S(2)}) copy-start(bf16[2,64,4,256]{3,2,1,0:T(4,128)(2,1)} %param.9) | copy-start | bytes 786436
  9.9 4.2 %copy-start.5 = (f32[4,256]{1,0:T(4,128)S(1)}, f32[4,256]{1,0:T(4,128)}, u32[]{:S(2)}) copy-start(f32[4,256]{1,0:T(4,128)} %param.10) | copy-start | bytes 12292
  15.2 6.6 %copy-start.9 = (s32[2,128]{1,0:T(2,128)S(1)}, s32[2,128]{1,0:T(2,128)}, u32[]{:S(2)}) copy-start(s32[2,128]{1,0:T(2,128)} %param.11) | copy-start | bytes 3076
  15.9 6.4 %collective-permute-start.1 = (bf16[129,1,256]{2,0,1:T(8,128)(2,1)}, bf16[129,1,256]{2,0,1:T(8,128)(2,1)S(1)}, u32[]{:S(2)}, u32[]{:S(2)}) collective-permute-start(bf16[129,1,256]{2,0,1:T(8,128)(2,1)} %get-tuple-element.23), channel_id=1, source_target_pairs={{8,0},{16,8},{24,16},{0,24},{9,1},{17,9},{25,17},{1,25},{10,2},{18... | collective-permute-start | bytes 198152 | tf_op jit(solution)/shard_map/ppermute | solution.py:19
  19.8 5.2 %collective-permute-start = (bf16[129,1,256]{2,0,1:T(8,128)(2,1)S(1)}, bf16[129,1,256]{2,0,1:T(8,128)(2,1)S(1)}, u32[]{:S(2)}, u32[]{:S(2)}) collective-permute-start(bf16[129,1,256]{2,0,1:T(8,128)(2,1)S(1)} %get-tuple-element.22), channel_id=1, source_target_pairs={{0,8},{8,16},{16,24},{24,0},{1,9},{9,17},{17,25},{25,1},{2,10},{10... | collective-permute-start | bytes 198152 | tf_op jit(solution)/shard_map/ppermute | solution.py:18
  25.4 2.8 %copy-start.3 = (f32[129,1,256]{0,1,2:T(1,128)}, f32[129,1,256]{0,1,2:T(1,128)S(1)}, u32[]{:S(2)}) copy-start(f32[129,1,256]{0,1,2:T(1,128)S(1)} %copy.58) | copy-start | bytes 396292
  26.6 3.5 %collective-permute-start.3 = (bf16[129,4,1]{0,1,2:T(4,128)(2,1)S(1)}, bf16[129,4,1]{0,1,2:T(4,128)(2,1)S(1)}, u32[]{:S(2)}, u32[]{:S(2)}) collective-permute-start(bf16[129,4,1]{0,1,2:T(4,128)(2,1)S(1)} %get-tuple-element.21), channel_id=1, source_target_pairs={{1,0},{2,1},{3,2},{4,3},{5,4},{6,5},{7,6},{0,7},{9,8},{10,9},{11,1... | collective-permute-start | bytes 3104 | tf_op jit(solution)/shard_map/ppermute | solution.py:19
  28.3 4.8 %collective-permute-start.2 = (bf16[129,4,1]{0,1,2:T(4,128)(2,1)S(1)}, bf16[129,4,1]{0,1,2:T(4,128)(2,1)S(1)}, u32[]{:S(2)}, u32[]{:S(2)}) collective-permute-start(bf16[129,4,1]{0,1,2:T(4,128)(2,1)S(1)} %get-tuple-element.20), channel_id=1, source_target_pairs={{0,1},{1,2},{2,3},{3,4},{4,5},{5,6},{6,7},{7,0},{8,9},{9,10},{10,1... | collective-permute-start | bytes 3104 | tf_op jit(solution)/shard_map/ppermute | solution.py:18
  39.2 1.2 %copy-start.2 = (f32[2,64,4,256]{1,0,3,2:T(2,128)S(1)}, f32[2,64,4,256]{1,0,3,2:T(2,128)}, u32[]{:S(2)}) copy-start(f32[2,64,4,256]{1,0,3,2:T(2,128)} %convert_element_type.68) | copy-start | bytes 1572868
  42.9 2.9 %copy-start.6 = (f32[2,4,1,1,1]{1,0,4,3,2:T(2,128)S(1)}, f32[2,4,1,1,1]{1,0,4,3,2:T(2,128)}, u32[]{:S(2)}) copy-start(f32[2,4,1,1,1]{1,0,4,3,2:T(2,128)} %constant.27) | copy-start | bytes 100
  45.8 6.3 %copy-start.10 = (bf16[256,1024]{1,0:T(8,128)(2,1)S(1)}, bf16[256,1024]{1,0:T(8,128)(2,1)}, u32[]{:S(2)}) copy-start(bf16[256,1024]{1,0:T(8,128)(2,1)} %param.12) | copy-start | bytes 1572868
where the time goes:
time: 55.3 us; the launch traced here: 54.9 us
  local copies, waits for them, and re-layouts  20.4 us (37%)
  other arithmetic  11.4 us (21%)
  matrix products  10.5 us (19%)
  waiting for transfers between devices  5.89 us (11%)
  starting transfers between devices  5.59 us (10%)
  between operations  1.06 us (2%)
    dot_general x2, matrix products, remap_columns(): jnp.einsum('pa,qb,...xayb->...xpyq', weights_table, weights_table, blocks...  5.77 us
    ppermute x2, waiting for transfers between devices, extended(): before = lax.ppermute(last, axis, up)  5.71 us
    ppermute x2, starting transfers between devices, extended(): after = lax.ppermute(leading, axis, down)  5.59 us
    unnamed x26, local copies, waits for them, and re-layouts  3.82 us
    add x1, other arithmetic, shards(): tracers_next = tracers + time_step * averaged.reshape(tracers.shape)  2.91 us
    another operation x1, local copies, waits for them, and re-layouts  2.89 us
    concatenate x1, other arithmetic, shards(): stacked = jnp.concatenate([tracers_next, winds.astype(jnp.float32)], axis=0)  2.49 us
    slice x4, local copies, waits for them, and re-layouts, shards(): averaged = summed[:-1] / summed[-1:]  2.37 us
  transfers between devices with their start and end apart: 4, of which 3 were waited for; matrix products, arithmetic and copies ran while one was open for 7% of the time, Pallas kernels for 0%

commit v1 on v0

v1 whole, which is shorter than its diff:
```python
import functools

import jax
import jax.numpy as jnp
import numpy as np
from jax import lax
from jax.experimental import pallas as pl
from jax.experimental.pallas import tpu as pltpu
from jax.sharding import PartitionSpec as P

MESH = pl.DeviceIdType.MESH
time_step = 0.02
remap_ints = ((9.0, 8.0, 3.0, 0.0), (0.0, 3.0, 8.0, 9.0))
gll_points = (-1.0, -0.4472135954999579, 0.4472135954999579, 1.0)

DIRS = ((1, 0), (-1, 0), (0, 1), (0, -1), (1, 1), (1, -1), (-1, 1), (-1, -1))
FROM_UP, FROM_DOWN, FROM_LEFT, FROM_RIGHT = 0, 1, 2, 3
FROM_UL, FROM_UR, FROM_DL, FROM_DR = 4, 5, 6, 7


def gll_matrix():
    points = gll_points
    matrix = np.zeros((4, 4))
    for i in range(4):
        for j in range(4):
            if i == j:
                matrix[i, i] = 2.0 * sum(
                    1.0 / (points[i] - points[k]) for k in range(4) if k != i
                )
            else:
                num = den = 1.0
                for k in range(4):
                    if k != i:
                        num *= points[i] - points[k]
                    if k != j:
                        den *= points[j] - points[k]
                matrix[i, j] = 2.0 * num / (den * (points[i] - points[j]))
    return matrix


def constants(across):
    elements = across // 4
    eye = np.eye(elements)
    along = np.kron(eye, gll_matrix().T).astype(np.float32)
    high = along.astype(jnp.bfloat16)
    low = (along - high.astype(np.float32)).astype(jnp.bfloat16)
    remap = np.kron(eye, np.array(remap_ints).T).astype(jnp.bfloat16)
    pick = np.zeros((4, 8, across), np.float32)
    for a in range(4):
        pick[a, a, 0] = 1.0
        pick[a, 4 + a, across - 1] = 1.0
    place = np.zeros((4, 48, across), np.float32)
    for a in range(4):
        place[a, 8 * 0 + 4 + a, 0] = 1.0
        place[a, 8 * 1 + a, across - 1] = 1.0
    place[0, 8 * 2 + 7, 0] = 1.0
    place[0, 8 * 3 + 3, across - 1] = 1.0
    place[3, 8 * 4 + 4, 0] = 1.0
    place[3, 8 * 5 + 0, across - 1] = 1.0
    return high, low, remap, pick.astype(jnp.bfloat16), place.astype(jnp.bfloat16)


def dot(a, b):
    return jnp.dot(a, b, preferred_element_type=jnp.float32)


def split(value):
    high = value.astype(jnp.bfloat16)
    return high, (value - high.astype(jnp.float32)).astype(jnp.bfloat16)


def kernel(
    sizes,
    tracers_ref, winds_ref, mass_ref, cost_ref, win_hbm, wout_hbm,
    dhigh_ref, dlow_ref, remap_ref, pick_ref, place_ref,
    next_ref, cols_ref,
    win, wout, win_t, wout_t, weighted, rows_out, rows_in, ends_out, ends_in,
    mass_in, state, local_sem, send_sem, recv_sem,
):
    n_grp, n_bal = sizes
    levels = winds_ref.shape[1] // 2
    across = winds_ref.shape[2]
    grp, bal = lax.axis_index("grp"), lax.axis_index("bal")

    def peer(i):
        dg, db = DIRS[i]
        return (lax.rem(grp + dg + n_grp, n_grp), lax.rem(bal + db + n_bal, n_bal))

    barrier = pltpu.get_barrier_semaphore()
    for i in range(8):
        pl.semaphore_signal(barrier, inc=1, device_id=peer(i), device_id_type=MESH)
    load_in = pltpu.make_async_copy(win_hbm, win, local_sem.at[0])
    load_out = pltpu.make_async_copy(wout_hbm, wout, local_sem.at[1])
    load_in.start()
    load_out.start()

    derivative = gll_matrix()

    def weigh(a):
        here = tracers_ref[a]
        high, low = split(here)
        along_y = dot(high, dhigh_ref[...]) + dot(low, dhigh_ref[...]) + dot(high, dlow_ref[...])
        along_x = sum(float(derivative[a, c]) * tracers_ref[c] for c in range(4))
        first = winds_ref[a, :levels, :].astype(jnp.float32)
        second = winds_ref[a, levels:, :].astype(jnp.float32)
        mass = mass_ref[a : a + 1, :]
        first, second = first * mass, second * mass
        for k in range(2):
            part = slice(k * levels, (k + 1) * levels)
            weighted[a, part, :] = -(first * along_x[part] + second * along_y[part])

    for a in (0, 3):
        weigh(a)
    rows_out[0] = weighted[3].astype(jnp.bfloat16)
    rows_out[1] = weighted[0].astype(jnp.bfloat16)

    pl.semaphore_wait(barrier, 8)
    copies = []

    def send(src, dst, slot, i):
        copy = pltpu.make_async_remote_copy(
            src_ref=src, dst_ref=dst, send_sem=send_sem.at[slot], recv_sem=recv_sem.at[slot],
            device_id=peer(i), device_id_type=MESH,
        )
        copy.start()
        copies.append(copy)
        return copy

    row_copies = [send(rows_out.at[i], rows_in.at[i], i, i) for i in range(2)]
    mass_copies = [send(mass_ref, mass_in.at[i], 2 + i, i) for i in range(8)]

    for a in (1, 2):
        weigh(a)
    ends = None
    for a in range(4):
        term = lax.dot_general(
            pick_ref[a], weighted[a].astype(jnp.bfloat16), (((1,), (1,)), ((), ())),
            preferred_element_type=jnp.float32,
        )
        ends = term if ends is None else ends + term
    ends_out[...] = ends

    lane = lax.broadcasted_iota(jnp.int32, (1, across), 1)
    takes_before = (lane % 4 == 0) & (lane > 0)
    takes_after = (lane % 4 == 3) & (lane < across - 1)

    half = across // 2
    winds_rows = 2 * levels
    for p in range(2):
        mixed = sum(
            remap_ints[p][a] * winds_ref[a].astype(jnp.float32)
            for a in range(4) if remap_ints[p][a]
        )
        high, low = split(mixed)
        cells = (dot(high, remap_ref[...]) + dot(low, remap_ref[...])) * (1.0 / 400.0)
        state[winds_rows:, p * half : (p + 1) * half] = cells.astype(jnp.bfloat16).astype(jnp.float32)

    end_copies = [send(ends_out, ends_in.at[i - 2], 8 + i, i) for i in range(2, 8)]

    load_in.wait()
    win_t[...] = win[...].T
    load_out.wait()
    wout_t[...] = wout[...].T

    for copy in mass_copies:
        copy.wait_recv()

    def join_rows(middle, upper, lower):
        return [middle[0:1] + upper[3:4], middle[1:2], middle[2:3], middle[3:4] + lower[0:1]]

    own = join_rows(mass_ref, mass_in[FROM_UP], mass_in[FROM_DOWN])
    left = join_rows(mass_in[FROM_LEFT], mass_in[FROM_UL], mass_in[FROM_DL])
    right = join_rows(mass_in[FROM_RIGHT], mass_in[FROM_UR], mass_in[FROM_DR])
    scales = []
    for a in range(4):
        before = pltpu.roll(jnp.where(lane == across - 1, left[a], own[a]), 1, 1)
        after = pltpu.roll(jnp.where(lane == 0, right[a], own[a]), across - 1, 1)
        total = own[a] + jnp.where(lane % 4 == 0, before, 0.0) + jnp.where(lane % 4 == 3, after, 0.0)
        scales.append(time_step / total)

    for copy in row_copies:
        copy.wait_recv()
    for copy in end_copies:
        copy.wait_recv()

    received = ends_in[...].reshape(48, ends_in.shape[-1]).astype(jnp.bfloat16)
    received = received.astype(jnp.float32).T.astype(jnp.bfloat16)
    mixed = [None, None]
    for a in range(4):
        value = weighted[a]
        if a == 0:
            value = value + rows_in[FROM_UP].astype(jnp.float32)
        if a == 3:
            value = value + rows_in[FROM_DOWN].astype(jnp.float32)
        before = pltpu.roll(value, 1, 1)
        after = pltpu.roll(value, across - 1, 1)
        total = value + jnp.where(takes_before, before, jnp.where(takes_after, after, 0.0))
        total = total + dot(received, place_ref[a])
        updated = tracers_ref[a] + scales[a] * total
        next_ref[a] = updated
        for p in range(2):
            if remap_ints[p][a]:
                term = remap_ints[p][a] * updated
                mixed[p] = term if mixed[p] is None else mixed[p] + term
    for p in range(2):
        high, low = split(mixed[p])
        cells = (dot(high, remap_ref[...]) + dot(low, remap_ref[...])) * (1.0 / 400.0)
        state[:winds_rows, p * half : (p + 1) * half] = cells.astype(jnp.bfloat16).astype(jnp.float32)

    cost = jnp.concatenate([cost_ref[0:1, :], cost_ref[1:2, :]], axis=1)
    hidden_size = win_t.shape[0]
    chunk = hidden_size // 4
    current = state[...]
    for step in range(3):
        inputs = current.astype(jnp.bfloat16)
        change = None
        for c in range(4):
            part = slice(c * chunk, (c + 1) * chunk)
            hidden = jax.nn.gelu(dot(win_t[part, :], inputs)).astype(jnp.bfloat16)
            term = dot(wout_t[:, part], hidden)
            change = term if change is None else change + term
        current = current + jnp.where(cost > step, change, 0.0)
    for p in range(2):
        cols_ref[p] = current[:, p * half : (p + 1) * half].astype(jnp.bfloat16)

    for copy in copies:
        copy.wait_send()


def shards(sizes, tracers, winds, node_mass, column_cost, weight_in, weight_out):
    levels, extent, across = tracers.shape[1:]
    features, hidden = weight_in.shape
    channels = 2 * levels
    rows = lambda x: x.transpose(2, 0, 1, 3).reshape(extent, channels, across)
    vmem = pl.BlockSpec(memory_space=pltpu.VMEM)
    hbm = pl.BlockSpec(memory_space=pl.ANY)
    f32, bf16 = jnp.float32, jnp.bfloat16
    next_rows, cols = pl.pallas_call(
        functools.partial(kernel, sizes),
        out_shape=(
            jax.ShapeDtypeStruct((extent, channels, across), f32),
            jax.ShapeDtypeStruct((2, features, across // 2), bf16),
        ),
        in_specs=[vmem] * 4 + [hbm] * 2 + [vmem] * 5,
        out_specs=(vmem, vmem),
        scratch_shapes=[
            pltpu.VMEM((features, hidden), bf16),
            pltpu.VMEM((hidden, features), bf16),
            pltpu.VMEM((hidden, features), bf16),
            pltpu.VMEM((features, hidden), bf16),
            pltpu.VMEM((extent, channels, across), f32),
            pltpu.VMEM((2, channels, across), bf16),
            pltpu.VMEM((2, channels, across), bf16),
            pltpu.VMEM((8, channels), f32),
            pltpu.VMEM((6, 8, channels), f32),
            pltpu.VMEM((8, extent, across), f32),
            pltpu.VMEM((features, across), f32),
            pltpu.SemaphoreType.DMA((2,)),
            pltpu.SemaphoreType.DMA((16,)),
            pltpu.SemaphoreType.DMA((16,)),
        ],
        compiler_params=pltpu.CompilerParams(collective_id=0, has_side_effects=True),
    )(
        rows(tracers), rows(winds), node_mass, column_cost, weight_in, weight_out,
        *constants(across),
    )
    tracers_next = next_rows.reshape(extent, 2, levels, across).transpose(1, 2, 0, 3)
    columns_out = cols.transpose(1, 0, 2).reshape(4, levels, 2, across // 2)
    return tracers_next, columns_out


def solution(mesh):
    grid = P(None, None, "grp", "bal")
    flat = P("grp", "bal")
    sizes = (mesh.shape["grp"], mesh.shape["bal"])
    return jax.shard_map(
        functools.partial(shards, sizes),
        mesh=mesh,
        in_specs=(grid, grid, flat, flat, P(), P()),
        out_specs=(grid, grid),
        check_vma=False,
    )
```

time: 55.3 us -> 21.7 us (0.39)
  Pallas kernels: 0 us -> 15.3 us
  local copies, waits for them, and re-layouts: 20.4 us -> 5.62 us
  other arithmetic: 11.4 us -> 0 us
  matrix products: 10.5 us -> 0 us
  waiting for transfers between devices: 5.89 us -> 0 us
  starting transfers between devices: 5.59 us -> 0 us
    pallas_call x0 -> x1, Pallas kernels: none -> 15.3 us  [shards(): pl.pallas_call(functools.partial(kernel, sizes), out_shape=(jax.ShapeDtyp...]
    dot_general x7 -> x0, matrix products: 10.5 us -> none  [the longest x2 5.77 us: remap_columns(): jnp.einsum('pa,qb,...xayb->...xpyq', weights_table, weights_table, blocks...]
    ppermute x4 -> x0, waiting for transfers between devices: 5.89 us -> none  [the longest x2 5.71 us: extended(): before = lax.ppermute(last, axis, up)]
    ppermute x4 -> x0, starting transfers between devices: 5.59 us -> none  [the longest x2 5.59 us: extended(): after = lax.ppermute(leading, axis, down)]
    slice x15 -> x0, local copies, waits for them, and re-layouts: 5.29 us -> none  [the longest x4 2.37 us: shards(): averaged = summed[:-1] / summed[-1:]]
    concatenate x4 -> x0, other arithmetic: 4.71 us -> none  [the longest x1 2.49 us: shards(): stacked = jnp.concatenate([tracers_next, winds.astype(jnp.float32)], axis=0)]
    unnamed x26 -> x5, local copies, waits for them, and re-layouts: 3.82 us -> 0.8 us
    add x1 -> x0, other arithmetic: 2.91 us -> none  [shards(): tracers_next = tracers + time_step * averaged.reshape(tracers.shape)]
  transfers between devices with their start and end apart: 4 -> 0, of which waited for: 3 -> 0; matrix products, arithmetic and copies ran while one was open for 7% -> 0% of each run, Pallas kernels for 0% -> 0%
where the time goes in v1:
time: 21.7 us; the launch traced here: 21.5 us
  Pallas kernels  15.3 us (71%)
  local copies, waits for them, and re-layouts  5.62 us (26%)
  between operations  0.66 us (3%)
    pallas_call x1, Pallas kernels, shards(): pl.pallas_call(functools.partial(kernel, sizes), out_shape=(jax.ShapeDtyp...  15.3 us
    transpose x2, local copies, waits for them, and re-layouts, shards(): rows = lambda x: x.transpose(2, 0, 1, 3).reshape(extent, channels, across)  2.62 us
    reshape x1, local copies, waits for them, and re-layouts, shards(): next_rows.reshape(extent, 2, levels, across).transpose(1, 2, 0, 3)  2.21 us
    unnamed x5, local copies, waits for them, and re-layouts  0.8 us

profile of v1, /device:TPU:0, one launch (start us, length us, event | category | flops | bytes accessed | tf_op | source)
XLA Modules:
  0.0 21.5 jit_solution(15417932610162151550)
XLA Ops:
  0.6 0.0 copy-start
  0.6 1.7 %copy.14 = bf16[4,2,64,256]{3,2,1,0:T(8,128)(2,1)} copy(bf16[4,2,64,256]{3,0,2,1:T(4,128)(2,1)} %bitcast.16) | data formatting | bytes 524288 | tf_op jit(solution)/shard_map/transpose | solution.py:234
  2.4 0.0 copy-done
  2.4 0.9 %copy.13 = f32[4,2,64,256]{3,2,1,0:T(8,128)} copy(f32[4,2,64,256]{3,0,2,1:T(4,128)S(1)} %bitcast.13) | data formatting | bytes 1048576 | tf_op jit(solution)/shard_map/transpose | solution.py:234
  3.3 15.3 %shard_map.122 = (f32[4,128,256]{2,1,0:T(8,128)}, bf16[2,256,128]{2,1,0:T(8,128)(2,1)}) custom-call(f32[4,128,256]{2,1,0:T(8,128)} %bitcast.11, bf16[4,128,256]{2,1,0:T(8,128)(2,1)} %bitcast.12, f32[4,256]{1,0:T(4,128)} %mass_ref.1, s32[2,128]{1,0:T(2,128)} %cost_ref.1, bf16[256,1024]{1,0:T(8,128)(2,1)} %win_hbm.1, bf16[1024,256]{1,0:T(8,128)(2,1)} %wout_hbm.1, ...), custom_call_target="tpu_custom_call" | custom-call | tf_op jit(solution)/shard_map/pallas_call | solution.py:238
  18.5 0.0 copy-start.1
  18.5 2.2 %copy.18 = f32[4,2,64,256]{3,0,2,1:T(4,128)} copy(f32[4,2,64,256]{3,2,1,0:T(8,128)} %bitcast.14) | data formatting | bytes 1048576 | tf_op jit(solution)/shard_map/reshape | solution.py:267
  20.7 0.0 copy-done.1
  20.7 0.8 %copy.16 = bf16[4,64,2,128]{3,2,1,0:T(2,128)(2,1)} copy(bf16[4,64,2,128]{3,1,0,2:T(8,128)(2,1)S(1)} %bitcast.17) | data formatting | bytes 262144
Async XLA Ops:
  0.6 1.7 %copy-start = (f32[2,64,4,256]{3,2,1,0:T(4,128)S(1)}, f32[2,64,4,256]{3,2,1,0:T(4,128)}, u32[]{:S(2)}) copy-start(f32[2,64,4,256]{3,2,1,0:T(4,128)} %param.11) | copy-start | bytes 1572868
  18.5 2.2 %copy-start.1 = (bf16[2,256,128]{2,1,0:T(8,128)(2,1)S(1)}, bf16[2,256,128]{2,1,0:T(8,128)(2,1)}, u32[]{:S(2)}) copy-start(bf16[2,256,128]{2,1,0:T(8,128)(2,1)} %get-tuple-element.5) | copy-start | bytes 393220

commit v2 on v1

--- a/solution.py
+++ b/solution.py
@@ -71,15 +71,16 @@
 
 def kernel(
     sizes,
-    tracers_ref, winds_ref, mass_ref, cost_ref, win_hbm, wout_hbm,
+    tracers_hbm, winds_hbm, mass_hbm, cost_hbm, win_hbm, wout_hbm,
+    dhigh_hbm, dlow_hbm, remap_hbm, pick_hbm, place_hbm,
+    next_hbm, cols_ref,
+    tracers_ref, winds_ref, mass_ref, cost_ref, win, wout,
     dhigh_ref, dlow_ref, remap_ref, pick_ref, place_ref,
-    next_ref, cols_ref,
-    win, wout, win_t, wout_t, weighted, rows_out, rows_in, ends_out, ends_in,
-    mass_in, state, local_sem, send_sem, recv_sem,
+    win_t, wout_t, weighted, next_ref, rows_out, rows_in, ends_out, ends_in,
+    mass_in, local_sem, store_sem, send_sem, recv_sem,
 ):
     n_grp, n_bal = sizes
-    levels = winds_ref.shape[1] // 2
-    across = winds_ref.shape[2]
+    levels, across = winds_ref.shape[1], winds_ref.shape[3]
     grp, bal = lax.axis_index("grp"), lax.axis_index("bal")
 
     def peer(i):
@@ -89,20 +90,38 @@
     barrier = pltpu.get_barrier_semaphore()
     for i in range(8):
         pl.semaphore_signal(barrier, inc=1, device_id=peer(i), device_id_type=MESH)
-    load_in = pltpu.make_async_copy(win_hbm, win, local_sem.at[0])
-    load_out = pltpu.make_async_copy(wout_hbm, wout, local_sem.at[1])
-    load_in.start()
-    load_out.start()
+
+    def load(src, dst, slot):
+        copy = pltpu.make_async_copy(src, dst, local_sem.at[slot])
+        copy.start()
+        return copy
+
+    load_rows = [load(tracers_hbm.at[:, :, a, :], tracers_ref.at[a], a) for a in range(4)]
+    load_high = load(dhigh_hbm, dhigh_ref, 4)
+    load_low = load(dlow_hbm, dlow_ref, 5)
+    load_winds = load(winds_hbm, winds_ref, 6)
+    load_mass = load(mass_hbm, mass_ref, 7)
+    load_pick = load(pick_hbm, pick_ref, 8)
+    load_remap = load(remap_hbm, remap_ref, 9)
+    load_in = load(win_hbm, win, 10)
+    load_out = load(wout_hbm, wout, 11)
+    load_place = load(place_hbm, place_ref, 12)
+    load_cost = load(cost_hbm, cost_ref, 13)
+    for copy in (*load_rows, load_high, load_low, load_winds, load_mass):
+        copy.wait()
+
+    def tracer_row(a):
+        return tracers_ref[a].reshape(2 * levels, across)
 
     derivative = gll_matrix()
 
     def weigh(a):
-        here = tracers_ref[a]
+        here = tracer_row(a)
         high, low = split(here)
         along_y = dot(high, dhigh_ref[...]) + dot(low, dhigh_ref[...]) + dot(high, dlow_ref[...])
-        along_x = sum(float(derivative[a, c]) * tracers_ref[c] for c in range(4))
-        first = winds_ref[a, :levels, :].astype(jnp.float32)
-        second = winds_ref[a, levels:, :].astype(jnp.float32)
+        along_x = sum(float(derivative[a, c]) * tracer_row(c) for c in range(4))
+        first = winds_ref[0, :, a, :].astype(jnp.float32)
+        second = winds_ref[1, :, a, :].astype(jnp.float32)
         mass = mass_ref[a : a + 1, :]
         first, second = first * mass, second * mass
         for k in range(2):
@@ -131,6 +150,7 @@
 
     for a in (1, 2):
         weigh(a)
+    load_pick.wait()
     ends = None
     for a in range(4):
         term = lax.dot_general(
@@ -145,15 +165,23 @@
     takes_after = (lane % 4 == 3) & (lane < across - 1)
 
     half = across // 2
-    winds_rows = 2 * levels
-    for p in range(2):
-        mixed = sum(
-            remap_ints[p][a] * winds_ref[a].astype(jnp.float32)
-            for a in range(4) if remap_ints[p][a]
-        )
+    load_remap.wait()
+
+    def cells_of(mixed):
         high, low = split(mixed)
         cells = (dot(high, remap_ref[...]) + dot(low, remap_ref[...])) * (1.0 / 400.0)
-        state[winds_rows:, p * half : (p + 1) * half] = cells.astype(jnp.bfloat16).astype(jnp.float32)
+        return cells.astype(jnp.bfloat16).astype(jnp.float32)
+
+    winds_cells = [
+        [
+            cells_of(sum(
+                remap_ints[p][a] * winds_ref[k, :, a, :].astype(jnp.float32)
+                for a in range(4) if remap_ints[p][a]
+            ))
+            for p in range(2)
+        ]
+        for k in range(2)
+    ]
 
     end_copies = [send(ends_out, ends_in.at[i - 2], 8 + i, i) for i in range(2, 8)]
 
@@ -178,6 +206,8 @@
         total = own[a] + jnp.where(lane % 4 == 0, before, 0.0) + jnp.where(lane % 4 == 3, after, 0.0)
         scales.append(time_step / total)
 
+    load_place.wait()
+    load_cost.wait()
     for copy in row_copies:
         copy.wait_recv()
     for copy in end_copies:
@@ -186,6 +216,7 @@
     received = ends_in[...].reshape(48, ends_in.shape[-1]).astype(jnp.bfloat16)
     received = received.astype(jnp.float32).T.astype(jnp.bfloat16)
     mixed = [None, None]
+    stores = []
     for a in range(4):
         value = weighted[a]
         if a == 0:
@@ -196,21 +227,27 @@
         after = pltpu.roll(value, across - 1, 1)
         total = value + jnp.where(takes_before, before, jnp.where(takes_after, after, 0.0))
         total = total + dot(received, place_ref[a])
-        updated = tracers_ref[a] + scales[a] * total
-        next_ref[a] = updated
+        updated = tracer_row(a) + scales[a] * total
+        next_ref[a] = updated.reshape(2, levels, across)
+        store = pltpu.make_async_copy(next_ref.at[a], next_hbm.at[:, :, a, :], store_sem.at[a])
+        store.start()
+        stores.append(store)
         for p in range(2):
             if remap_ints[p][a]:
                 term = remap_ints[p][a] * updated
                 mixed[p] = term if mixed[p] is None else mixed[p] + term
-    for p in range(2):
-        high, low = split(mixed[p])
-        cells = (dot(high, remap_ref[...]) + dot(low, remap_ref[...])) * (1.0 / 400.0)
-        state[:winds_rows, p * half : (p + 1) * half] = cells.astype(jnp.bfloat16).astype(jnp.float32)
+    current = jnp.concatenate(
+        [
+            jnp.concatenate([cells_of(mixed[p]) for p in range(2)], axis=1),
+            jnp.concatenate(winds_cells[0], axis=1),
+            jnp.concatenate(winds_cells[1], axis=1),
+        ],
+        axis=0,
+    )
 
     cost = jnp.concatenate([cost_ref[0:1, :], cost_ref[1:2, :]], axis=1)
     hidden_size = win_t.shape[0]
     chunk = hidden_size // 4
-    current = state[...]
     for step in range(3):
         inputs = current.astype(jnp.bfloat16)
         change = None
@@ -220,9 +257,10 @@
             term = dot(wout_t[:, part], hidden)
             change = term if change is None else change + term
         current = current + jnp.where(cost > step, change, 0.0)
-    for p in range(2):
-        cols_ref[p] = current[:, p * half : (p + 1) * half].astype(jnp.bfloat16)
-
+    cols_ref[...] = jnp.stack([current[:, :half], current[:, half:]], axis=1).astype(jnp.bfloat16)
+
+    for copy in stores:
+        copy.wait()
     for copy in copies:
         copy.wait_send()
 
@@ -231,42 +269,44 @@
     levels, extent, across = tracers.shape[1:]
     features, hidden = weight_in.shape
     channels = 2 * levels
-    rows = lambda x: x.transpose(2, 0, 1, 3).reshape(extent, channels, across)
     vmem = pl.BlockSpec(memory_space=pltpu.VMEM)
     hbm = pl.BlockSpec(memory_space=pl.ANY)
     f32, bf16 = jnp.float32, jnp.bfloat16
-    next_rows, cols = pl.pallas_call(
+    rows = (extent, 2, levels, across)
+    tables = constants(across)
+    tracers_next, cols = pl.pallas_call(
         functools.partial(kernel, sizes),
         out_shape=(
-            jax.ShapeDtypeStruct((extent, channels, across), f32),
-            jax.ShapeDtypeStruct((2, features, across // 2), bf16),
+            jax.ShapeDtypeStruct(tracers.shape, f32),
+            jax.ShapeDtypeStruct((features, 2, across // 2), bf16),
         ),
-        in_specs=[vmem] * 4 + [hbm] * 2 + [vmem] * 5,
-        out_specs=(vmem, vmem),
+        in_specs=[hbm] * 11,
+        out_specs=(hbm, vmem),
         scratch_shapes=[
+            pltpu.VMEM(rows, f32),
+            pltpu.VMEM(winds.shape, bf16),
+            pltpu.VMEM(node_mass.shape, f32),
+            pltpu.VMEM(column_cost.shape, jnp.int32),
             pltpu.VMEM((features, hidden), bf16),
             pltpu.VMEM((hidden, features), bf16),
+            *[pltpu.VMEM(table.shape, bf16) for table in tables],
             pltpu.VMEM((hidden, features), bf16),
             pltpu.VMEM((features, hidden), bf16),
             pltpu.VMEM((extent, channels, across), f32),
+            pltpu.VMEM(rows, f32),
             pltpu.VMEM((2, channels, across), bf16),
             pltpu.VMEM((2, channels, across), bf16),
             pltpu.VMEM((8, channels), f32),
             pltpu.VMEM((6, 8, channels), f32),
             pltpu.VMEM((8, extent, across), f32),
-            pltpu.VMEM((features, across), f32),
-            pltpu.SemaphoreType.DMA((2,)),
+            pltpu.SemaphoreType.DMA((14,)),
+            pltpu.SemaphoreType.DMA((4,)),
             pltpu.SemaphoreType.DMA((16,)),
             pltpu.SemaphoreType.DMA((16,)),
         ],
         compiler_params=pltpu.CompilerParams(collective_id=0, has_side_effects=True),
-    )(
-        rows(tracers), rows(winds), node_mass, column_cost, weight_in, weight_out,
-        *constants(across),
-    )
-    tracers_next = next_rows.reshape(extent, 2, levels, across).transpose(1, 2, 0, 3)
-    columns_out = cols.transpose(1, 0, 2).reshape(4, levels, 2, across // 2)
-    return tracers_next, columns_out
+    )(tracers, winds, node_mass, column_cost, weight_in, weight_out, *tables)
+    return tracers_next, cols.reshape(4, levels, 2, across // 2)
 
 
 def solution(mesh):

time: 21.7 us -> 18.9 us (0.87)
  local copies, waits for them, and re-layouts: 5.62 us -> 2.56 us
    transpose x2 -> x0, local copies, waits for them, and re-layouts: 2.62 us -> none  [shards(): rows = lambda x: x.transpose(2, 0, 1, 3).reshape(extent, channels, across)]
    reshape x1 -> x0, local copies, waits for them, and re-layouts: 2.21 us -> none  [shards(): next_rows.reshape(extent, 2, levels, across).transpose(1, 2, 0, 3)]
    unnamed x5 -> x4, local copies, waits for them, and re-layouts: 0.8 us -> 2.56 us
    pallas_call x1, Pallas kernels: 15.3 us -> 15.5 us  [shards(): pl.pallas_call(functools.partial(kernel, sizes), out_shape=(jax.ShapeDtyp...]
where the time goes in v2:
time: 18.9 us; the launch traced here: 18.7 us
  Pallas kernels  15.5 us (82%)
  local copies, waits for them, and re-layouts  2.56 us (14%)
  between operations  0.65 us (3%)
    pallas_call x1, Pallas kernels, shards(): pl.pallas_call(functools.partial(kernel, sizes), out_shape=(jax.ShapeDtyp...  15.5 us
    unnamed x4, local copies, waits for them, and re-layouts  2.56 us

profile of v2, /device:TPU:0, one launch (start us, length us, event | category | flops | bytes accessed | tf_op | source)
XLA Modules:
  0.0 18.7 jit_solution(1025804879025932960)
XLA Ops:
  0.6 15.5 %shard_map.122 = (f32[2,64,4,256]{3,2,1,0:T(4,128)}, bf16[256,2,128]{2,1,0:T(2,128)(2,1)}) custom-call(f32[2,64,4,256]{3,2,1,0:T(4,128)} %tracers_hbm.1, bf16[2,64,4,256]{3,2,1,0:T(4,128)(2,1)} %winds_hbm.1, f32[4,256]{1,0:T(4,128)} %mass_hbm.1, s32[2,128]{1,0:T(2,128)} %cost_hbm.1, bf16[256,1024]{1,0:T(8,128)(2,1)} %win_hbm.1, bf16[1024,256]{1,0:T(8,128)(2,1)} %wout_hbm.1, ...), custom_call_target="tpu_custom_call" | custom-call | tf_op jit(solution)/shard_map/pallas_call | solution.py:277
  16.1 0.0 copy-start
  16.1 1.9 %copy.15 = f32[2,64,4,256]{3,2,1,0:T(4,128)} copy(f32[2,64,4,256]{3,2,1,0:T(4,128)} %get-tuple-element.8) | data formatting | bytes 1048576
  18.1 0.0 copy-done
  18.1 0.7 %copy.16 = bf16[4,64,2,128]{3,2,1,0:T(2,128)(2,1)} copy(bf16[4,64,2,128]{3,2,1,0:T(2,128)(2,1)S(1)} %bitcast.1) | data formatting | bytes 262144
Async XLA Ops:
  16.1 1.9 %copy-start = (bf16[256,2,128]{2,1,0:T(2,128)(2,1)S(1)}, bf16[256,2,128]{2,1,0:T(2,128)(2,1)}, u32[]{:S(2)}) copy-start(bf16[256,2,128]{2,1,0:T(2,128)(2,1)} %get-tuple-element.5) | copy-start | bytes 393220
